TPU v7x, 32 devices: a whole 2x2x4 slice. The times are simulated.
32 devices in a mesh: ctx: 2 (over x), tp: 4 (over y, core), dp: 4 (over z).
Axes of the slice: x: 2, y: 2, z: 4, core: 2. Of those that a mesh axis runs over, the one named last changes fastest.
Arguments:
- hidden: bfloat16 [4, 1024, 4096], P('dp', 'ctx', 'tp'), may hold values from -6 to 6
- target: bfloat16 [4, 1024, 4096], P('dp', 'ctx', 'tp'), may hold values from -24 to 24
- gain: float32 [4096], replicated, may hold values from 0.5 to 1.5
- w_query: bfloat16 [4096, 2048], P(('ctx', 'dp'), 'tp'), may hold values from -2.15625 to 2.15625
- w_key: bfloat16 [4096, 512], P(('ctx', 'dp'), 'tp'), may hold values from -0.09375 to 0.09375
- value_matrix: bfloat16 [4096, 512], P(('ctx', 'dp'), 'tp'), may hold values from -0.09375 to 0.09375
- w_out: bfloat16 [2048, 4096], P('tp', ('ctx', 'dp')), may hold values from -0.125 to 0.125
- block_order: int32 [4], replicated, may hold values from 0 to 3, each once
Outputs:
- branch: bfloat16 [4, 1024, 4096], P('dp', 'ctx', 'tp')
- loss: float32 [], replicated
Inputs may be any that keep to these rules, and one draw needn't show every extreme that they name: block_order is a permutation of 0 to 3.
All inputs are finite; a program needn't handle non-finite values.
Results may differ from a plain program's by a relative error of at most 0.013.
The roundings to bfloat16 on the way count: a program that leaves them out, or rounds other values in their place, can miss the bound.
Values may be sent and summed in bfloat16 or wider, within the bound.
A program may use at most 128 MiB of HBM per device.

v0:
```python
import jax
import jax.numpy as jnp
from jax import lax
from jax.sharding import PartitionSpec as P

MODEL_WIDTH = 4096
QUERY_HEADS = 16
KEY_VALUE_HEADS = 4
HEAD_SIZE = 128


rope_base = 500000.0


def shifted(value, axis, by):
    peers = lax.axis_size(axis)
    return lax.ppermute(value, axis, [(i, (i + by) % peers) for i in range(peers)])


def positions(order, start, rows, half):
    index = start + lax.iota(jnp.int32, rows)
    block = index // half
    slots = lax.iota(jnp.int32, order.shape[0])
    chosen = jnp.sum(jnp.where(block[:, None] == slots[None, :], order[None, :], 0), axis=1)
    return chosen * half + index % half


def apply_rotary(values, token_places):
    half = values.shape[-1] // 2
    freqs = rope_base ** (-(jnp.arange(half, dtype=jnp.float32) * 2.0) / values.shape[-1])
    angles = token_places.astype(jnp.float32)[:, None] * freqs[None, :]
    cosine = jnp.cos(angles)[:, None, :]
    sine = jnp.sin(angles)[:, None, :]
    first = values[..., :half]
    second = values[..., half:]
    return jnp.concatenate(
        [first * cosine - second * sine, second * cosine + first * sine], axis=-1
    )


def attend(state, query_rows, qpos, piece, kpos):
    peak, total, accum = state
    rows = piece.shape[1]
    local_heads = query_rows.shape[1]
    pair = piece.reshape(2, rows, local_heads, HEAD_SIZE)
    scores = jnp.einsum(
        "qcgd,kcd->cgqk", query_rows, pair[0], preferred_element_type=jnp.float32
    ) * (1.0 / HEAD_SIZE**0.5)
    allowed = (qpos[:, None] >= kpos[None, :])[None, None]
    scores = jnp.where(allowed, scores, -1e30)
    new_peak = jnp.maximum(peak, jnp.max(scores, axis=-1))
    weights = jnp.where(allowed, jnp.exp(scores - new_peak[..., None]), 0.0)
    factor = jnp.exp(peak - new_peak)
    total = total * factor + jnp.sum(weights, axis=-1)
    update = jnp.einsum(
        "cgqk,kcd->qcgd", weights.astype(jnp.bfloat16), pair[1], preferred_element_type=jnp.float32
    )
    accum = accum * jnp.transpose(factor, (2, 0, 1))[..., None] + update
    return (new_peak, total, accum)


def on_device(hidden, target, gain, w_query, w_key, value_matrix, w_out, block_order):
    rows = hidden.shape[1]
    half = rows // 2
    local = hidden[0]
    whole = lax.all_gather(local, "tp", axis=1, tiled=True)
    wide = whole.astype(jnp.float32)
    normed = (
        wide * lax.rsqrt(jnp.mean(wide * wide, axis=1, keepdims=True) + 1e-05) * gain[None, :]
    ).astype(jnp.bfloat16)
    pieces = (
        lax.all_gather(w_query, ("ctx", "dp"), axis=0, tiled=True),
        lax.all_gather(w_key, ("ctx", "dp"), axis=0, tiled=True),
        lax.all_gather(value_matrix, ("ctx", "dp"), axis=0, tiled=True),
    )
    query_rows, key, value_rows = tuple(
        (jnp.dot(normed, piece, preferred_element_type=jnp.float32) for piece in pieces)
    )
    shard = lax.axis_index("ctx")
    qpos = positions(block_order, shard * rows, rows, half)
    local_heads = w_key.shape[1] // HEAD_SIZE
    query_group = QUERY_HEADS // KEY_VALUE_HEADS
    query_rows = (
        apply_rotary(query_rows.reshape(rows, local_heads * query_group, HEAD_SIZE), qpos)
        .astype(jnp.bfloat16)
        .reshape(rows, local_heads, query_group, HEAD_SIZE)
    )
    key = (
        apply_rotary(key.reshape(rows, local_heads, HEAD_SIZE), qpos)
        .astype(jnp.bfloat16)
        .reshape(rows, local_heads * HEAD_SIZE)
    )
    pair = jnp.stack([key, value_rows.astype(jnp.bfloat16)])
    state = (
        jnp.full((local_heads, query_group, rows), -1e30, jnp.float32),
        jnp.zeros((local_heads, query_group, rows), jnp.float32),
        jnp.zeros((rows, local_heads, query_group, HEAD_SIZE), jnp.float32),
    )
    count = lax.axis_size("ctx")
    state = attend(state, query_rows, qpos, pair, qpos)

    def turn(step, carry):
        moved, inner = carry
        moved = shifted(moved, "ctx", 1)
        source = (shard - step) % count
        return (
            moved,
            attend(
                inner, query_rows, qpos, moved, positions(block_order, source * rows, rows, half)
            ),
        )

    moved_end, state = lax.fori_loop(1, count, turn, (pair, state))
    peak, total, accum = state
    attn = (
        (accum / jnp.transpose(total, (2, 0, 1))[..., None])
        .astype(jnp.bfloat16)
        .reshape(rows, local_heads * query_group * HEAD_SIZE)
    )
    terms = jnp.dot(
        attn,
        lax.all_gather(w_out, ("ctx", "dp"), axis=1, tiled=True),
        preferred_element_type=jnp.float32,
    )
    summed = lax.psum_scatter(terms.astype(jnp.bfloat16), "tp", scatter_dimension=1, tiled=True)
    resid = local.astype(jnp.float32) + summed.astype(jnp.float32) - target[0].astype(jnp.float32)
    squares = lax.psum(jnp.sum(resid * resid), ("ctx", "tp", "dp"))
    loss = squares / (lax.axis_size("dp") * lax.axis_size("ctx") * rows * MODEL_WIDTH)
    return (summed[None], loss)


def solution(mesh):
    in_specs = (
        P("dp", "ctx", "tp"),
        P("dp", "ctx", "tp"),
        P(),
        P(("ctx", "dp"), "tp"),
        P(("ctx", "dp"), "tp"),
        P(("ctx", "dp"), "tp"),
        P("tp", ("ctx", "dp")),
        P(),
    )
    out_specs = (P("dp", "ctx", "tp"), P())
    return jax.shard_map(
        on_device, mesh=mesh, in_specs=in_specs, out_specs=out_specs, check_vma=False
    )
```

profile of v0, /device:TPU:0, one launch (start us, length us, event | category | flops | bytes accessed | tf_op | source)
XLA Modules:
  0.0 378.8 jit_solution(6131819200116777629)
XLA Ops:
  8.0 0.7 all-gather.7.cloned.1.call-update
  10.7 0.7 select_reduce_fusion
  11.4 1.8 multiply_cosine_fusion
  13.6 33.2 %all-gather.15.cloned.1.call-done = bf16[1,512,4096]{2,1,0:T(8,128)(2,1)} async-done(((bf16[1,512,1024]{2,1,0:T(8,128)(2,1)}), bf16[1,512,4096]{2,1,0:T(8,128)(2,1)}) %all-gather.15.cloned.1.call-update) | async-done | bytes 4194320 | tf_op jit(solution)/shard_map/all_gather | solution.py:66
  46.8 3.1 fusion
  49.9 39.3 %all-gather.7.cloned.1.call-done = bf16[4096,128]{1,0:T(8,128)(2,1)} async-done(((bf16[512,128]{1,0:T(8,128)(2,1)}), bf16[4096,128]{1,0:T(8,128)(2,1)}) %all-gather.7.cloned.1.call-update) | async-done | bytes 1048592 | tf_op jit(solution)/shard_map/all_gather | solution.py:73
  89.2 4.1 %convolution_bitcast_fusion = f32[512,1,128]{0,2,1:T(8,128)S(1)} fusion(bf16[4096,128]{1,0:T(8,128)(2,1)} %all-gather.7.cloned.1.call-done, bf16[1,512,4096]{2,1,0:T(8,128)(2,1)} %all-gather.15.cloned.1.call-done, f32[4096]{0:T(1024)S(1)} %copy-done.4, f32[512]{0:T(512)S(1)} %add_rsqrt_fusion), kind=kOutput, calls=%fused_computation.31 | convolution fusion | flops 545259520 | bytes 5523456 | tf_op jit(solution)/shard_map/dot_general | solution.py:77
  93.9 36.5 %all-gather.11.cloned.1.call-done = bf16[4096,128]{1,0:T(8,128)(2,1)} async-done(((bf16[512,128]{1,0:T(8,128)(2,1)}), bf16[4096,128]{1,0:T(8,128)(2,1)}) %all-gather.11.cloned.1.call-update) | async-done | bytes 1048592 | tf_op jit(solution)/shard_map/all_gather | solution.py:74
  130.4 4.1 %convolution_convert_fusion.1 = bf16[512,128]{0,1:T(8,128)(2,1)S(1)} fusion(bf16[4096,128]{1,0:T(8,128)(2,1)} %all-gather.11.cloned.1.call-done, bf16[1,512,4096]{2,1,0:T(8,128)(2,1)} %all-gather.15.cloned.1.call-done, f32[4096]{0:T(1024)S(1)} %copy-done.4, f32[512]{0:T(512)S(1)} %add_rsqrt_fusion), kind=kOutput, calls=%fused_computation.32 | convolution fusion | flops 545325056 | bytes 5392384 | tf_op jit(solution)/shard_map/dot_general | solution.py:77
  134.5 0.8 pad_maximum_fusion.1
  135.9 68.1 %all-gather.9.cloned.1.call-done = bf16[4096,512]{1,0:T(8,128)(2,1)} async-done(((bf16[512,512]{1,0:T(8,128)(2,1)}), bf16[4096,512]{1,0:T(8,128)(2,1)}) %all-gather.9.cloned.1.call-update) | async-done | bytes 4194320 | tf_op jit(solution)/shard_map/all_gather | solution.py:72
  203.9 5.9 %fusion.74 = f32[512,512]{0,1:T(8,128)S(1)} fusion(bf16[4096,512]{1,0:T(8,128)(2,1)} %all-gather.9.cloned.1.call-done, bf16[1,512,4096]{2,1,0:T(8,128)(2,1)} %all-gather.15.cloned.1.call-done, f32[4096]{0:T(1024)S(1)} %copy-done.4, f32[512]{0:T(512)S(1)} %add_rsqrt_fusion), kind=kOutput, calls=%fused_computation.109 | convolution fusion | flops 2155872256 | bytes 9455616 | tf_op jit(solution)/shard_map/dot_general | solution.py:77
  210.6 1.2 subtract_convert_fusion
  211.9 1.2 fusion.3
  213.1 2.1 fusion.4
  215.3 1.0 fusion.5
  216.3 1.2 fusion.7
  217.6 1.3 fusion.28
  218.9 2.2 divide_convert_fusion
  221.1 57.8 %all-gather.13.cloned.1.call-done = bf16[512,4096]{1,0:T(8,128)(2,1)} async-done(((bf16[512,512]{1,0:T(8,128)(2,1)}), bf16[512,4096]{1,0:T(8,128)(2,1)}) %all-gather.13.cloned.1.call-update) | async-done | bytes 4194320 | tf_op jit(solution)/shard_map/all_gather | solution.py:122
  279.0 6.5 %convolution_convert_fusion = bf16[512,4096]{1,0:T(8,128)(2,1)} fusion(bf16[512,512]{0,1:T(8,128)(2,1)S(1)} %bitcast.172, bf16[512,4096]{1,0:T(8,128)(2,1)} %all-gather.13.cloned.1.call-done), kind=kOutput, calls=%fused_computation.5 | convolution fusion | flops 2149580800 | bytes 8912896 | tf_op jit(solution)/shard_map/dot_general | solution.py:120
  285.6 42.7 %reduce-scatter.2.cloned.1.call-done = bf16[512,1024]{1,0:T(8,128)(2,1)} async-done(((bf16[512,4096]{1,0:T(8,128)(2,1)}), bf16[512,1024]{1,0:T(8,128)(2,1)}) %reduce-scatter.2.cloned.1.call-update) | async-done | bytes 1048592 | tf_op jit(solution)/shard_map/reduce_scatter | solution.py:125
  328.3 2.4 fusion.12
  330.7 39.5 %psum.7 = f32[]{:T(128)} all-reduce(f32[]{:T(128)} %fusion.12), channel_id=1, replica_groups=mesh['ctx'=2,'tp'=4,'dp'=4] {'ctx','tp','dp'}, use_global_device_ids=true, to_apply=%region_9.10 | all-reduce | flops 1 | bytes 8 | tf_op jit(solution)/shard_map/psum | solution.py:127
  (35 shorter events, 5.0 us)
Async XLA Ops:
  7.2 82.0 %copy-start.4 = (f32[4096]{0:T(1024)S(1)}, f32[4096]{0:T(1024)}, u32[]{:S(2)}) copy-start(f32[4096]{0:T(1024)} %param.10) | copy-start | bytes 49156
  7.2 39.6 %all-gather.15.cloned.1.call-start = ((), (), s32[]{:S(2)}) async-start(), calls=%async_computation.6 | async-start | bytes 5242880 | tf_op jit(solution)/shard_map/all_gather | solution.py:66
  7.9 81.3 %all-gather.7.cloned.1.call-start = ((), (), s32[]{:S(2)}) async-start(), calls=%async_computation.1 | async-start | bytes 1179648 | tf_op jit(solution)/shard_map/all_gather | solution.py:73
  8.7 121.8 %all-gather.11.cloned.1.call-start = ((), (), s32[]{:S(2)}) async-start(), calls=%async_computation.3 | async-start | bytes 1179648 | tf_op jit(solution)/shard_map/all_gather | solution.py:74
  9.4 194.5 %all-gather.9.cloned.1.call-start = ((), (), s32[]{:S(2)}) async-start(), calls=%async_computation.2 | async-start | bytes 4718592 | tf_op jit(solution)/shard_map/all_gather | solution.py:72
  10.0 269.0 %all-gather.13.cloned.1.call-start = ((), (), s32[]{:S(2)}) async-start(), calls=%async_computation.4 | async-start | bytes 4718592 | tf_op jit(solution)/shard_map/all_gather | solution.py:122
  10.6 317.7 %reduce-scatter.2.cloned.1.call-start = ((), (), s32[]{:S(2)}) async-start(), calls=%async_computation.5 | async-start | bytes 5242880 | tf_op jit(solution)/shard_map/reduce_scatter | solution.py:125
  134.5 1.4 copy-start.2
  135.3 77.8 %collective-permute-start = (bf16[2,512,128]{1,2,0:T(8,128)(2,1)}, bf16[2,512,128]{1,2,0:T(8,128)(2,1)}, u32[]{:S(2)}, u32[]{:S(2)}) collective-permute-start(bf16[2,512,128]{1,2,0:T(8,128)(2,1)} %pad_maximum_fusion.1), channel_id=1, source_target_pairs={{0,16},{16,0},{1,17},{17,1},{2,18},{18,2},{3,19},{19,3},{4,20},{20... | collective-permute-start | bytes 786440 | tf_op jit(solution)/shard_map/while/body/eval_jaxpr/ppermute | solution.py:17
  215.2 2.3 copy-start.3
  285.5 42.8 %copy-start = (bf16[1,512,1024]{2,1,0:T(8,128)(2,1)S(1)}, bf16[1,512,1024]{2,1,0:T(8,128)(2,1)}, u32[]{:S(2)}) copy-start(bf16[1,512,1024]{2,1,0:T(8,128)(2,1)} %param.8) | copy-start | bytes 3145732
  285.5 42.8 %copy-start.1 = (bf16[1,512,1024]{2,1,0:T(8,128)(2,1)S(1)}, bf16[1,512,1024]{2,1,0:T(8,128)(2,1)}, u32[]{:S(2)}) copy-start(bf16[1,512,1024]{2,1,0:T(8,128)(2,1)} %param.9) | copy-start | bytes 3145732
Sparse Core Ops, SparseCore 0:
  9.5 37.1 all-gather.14
  48.9 40.2 all-gather.6
  91.3 39.0 all-gather.10
  132.4 71.5 all-gather.8
  205.8 73.1 all-gather.12
  285.7 42.5 reduce-scatter.1
where the time goes:
time: 379 us
  waiting for transfers between devices  281 us (74%)
  blocking collectives  39.5 us (10%)
  matrix products  27.6 us (7%)
  between operations  16.1 us (4%)
  other arithmetic  13.3 us (4%)
    all_gather x1, waiting for transfers between devices, on_device(): lax.all_gather(w_query, ('ctx', 'dp'), axis=0, tiled=True)  68.1 us
    all_gather x1, waiting for transfers between devices, on_device(): lax.all_gather(w_out, ('ctx', 'dp'), axis=1, tiled=True)  57.8 us
    reduce_scatter x1, waiting for transfers between devices, on_device(): lax.psum_scatter(terms.astype(jnp.bfloat16), 'tp', scatter_dimension=1, t...  42.7 us
    psum x1, blocking collectives, on_device(): squares = lax.psum(jnp.sum(resid * resid), ('ctx', 'tp', 'dp'))  39.5 us
    all_gather x1, waiting for transfers between devices, on_device(): lax.all_gather(w_key, ('ctx', 'dp'), axis=0, tiled=True)  39.3 us
    all_gather x1, waiting for transfers between devices, on_device(): lax.all_gather(value_matrix, ('ctx', 'dp'), axis=0, tiled=True)  36.5 us
    all_gather x1, waiting for transfers between devices, on_device(): whole = lax.all_gather(local, 'tp', axis=1, tiled=True)  33.2 us
    dot_general x3, matrix products, on_device(): jnp.dot(normed, piece, preferred_element_type=jnp.float32)  14.1 us
  transfers between devices with their start and end apart: 7, of which 6 were waited for; matrix products, arithmetic and copies ran while one was open for 9% of the time, Pallas kernels for 0%

commit v1 on v0

--- a/solution.py
+++ b/solution.py
@@ -1,6 +1,10 @@
+import functools
+
 import jax
 import jax.numpy as jnp
 from jax import lax
+from jax.experimental import pallas as pl
+from jax.experimental.pallas import tpu as pltpu
 from jax.sharding import PartitionSpec as P
 
 MODEL_WIDTH = 4096
@@ -129,6 +133,568 @@
     return (summed[None], loss)
 
 
+MESH = pl.DeviceIdType.MESH
+F32 = jnp.float32
+BF16 = jnp.bfloat16
+
+
+def layer(
+    nd,
+    order,
+    hidden,
+    target,
+    gain,
+    freqs,
+    w_query,
+    w_key,
+    value_matrix,
+    w_out,
+    out,
+    loss,
+    ga,
+    go,
+    xs,
+    goal,
+    normed,
+    acc,
+    trig,
+    query,
+    kv,
+    attn,
+    kept,
+    sent,
+    sib,
+    ysend,
+    yrecv,
+    tile,
+    sums_tp,
+    sums_all,
+    load_sem,
+    a_send,
+    a_recv,
+    o_send,
+    o_recv,
+    h_send,
+    h_recv,
+    kv_send,
+    kv_recv,
+    s_send,
+    s_recv,
+    y_send,
+    y_recv,
+    t_send,
+    t_recv,
+    l_send,
+    l_recv,
+):
+    c, t, d = lax.axis_index("ctx"), lax.axis_index("tp"), lax.axis_index("dp")
+    nb = 2 * nd
+    me = c * nd + d
+    y, k = t // 2, t % 2
+    sibling = y * 2 + (1 - k)
+    across = (1 - y) * 2 + k
+    diagonal = (1 - y) * 2 + (1 - k)
+    rows, wide = hidden.shape
+    deep = w_query.shape[0]
+    qcols = w_query.shape[1]
+    half = rows // 2
+    n_heads = qcols // HEAD_SIZE
+    e = d + 1 - 2 * (d % 2)
+
+    loads = [
+        pltpu.make_async_copy(w_query, ga.at[me, :, pl.ds(0, qcols)], load_sem.at[0]),
+        pltpu.make_async_copy(w_key, ga.at[me, :, pl.ds(qcols, HEAD_SIZE)], load_sem.at[1]),
+        pltpu.make_async_copy(
+            value_matrix, ga.at[me, :, pl.ds(qcols + HEAD_SIZE, HEAD_SIZE)], load_sem.at[2]
+        ),
+        pltpu.make_async_copy(hidden, xs.at[t], load_sem.at[3]),
+        pltpu.make_async_copy(w_out, go.at[me], load_sem.at[4]),
+        pltpu.make_async_copy(target, goal, load_sem.at[5]),
+    ]
+    for load in loads:
+        load.start()
+
+    barrier = pltpu.get_barrier_semaphore()
+    for s in range(1, nb):
+        p = (me + s) % nb
+        pl.semaphore_signal(
+            barrier, inc=1, device_id={"ctx": p // nd, "dp": p % nd}, device_id_type=MESH
+        )
+    for s in (sibling, across, diagonal):
+        pl.semaphore_signal(barrier, inc=1, device_id={"tp": s}, device_id_type=MESH)
+    pl.semaphore_wait(barrier, nb + 2)
+
+    def remote(src, dst, ssem, rsem, where):
+        return pltpu.make_async_remote_copy(
+            src_ref=src, dst_ref=dst, send_sem=ssem, recv_sem=rsem,
+            device_id=where, device_id_type=MESH,
+        )
+
+    X, UP, DOWN = 0, 1, 2
+
+    def piece(buf, ssem, rsem, b, way):
+        where = {
+            X: {"ctx": 1 - c},
+            UP: {"dp": jnp.minimum(d + 1, nd - 1)},
+            DOWN: {"dp": jnp.maximum(d - 1, 0)},
+        }[way]
+        return remote(buf.at[b], buf.at[b], ssem.at[way, b], rsem.at[b], where)
+
+    def a_piece(b, way):
+        return piece(ga, a_send, a_recv, b, way)
+
+    def o_piece(b, way):
+        return piece(go, o_send, o_recv, b, way)
+
+    def block(src, j, dst, i, ssem, rsem, where):
+        return remote(src.at[j], dst.at[i], ssem, rsem, {"tp": where})
+
+    def h_copy(slot, i, where):
+        return block(xs, slot, xs, slot, h_send.at[i], h_recv.at[i], where)
+
+    h_sib = h_copy(t, 0, sibling)
+    h_across = h_copy(t, 1, across)
+    h_relay = h_copy(across, 2, sibling)
+    for i in range(3):
+        loads[i].wait()
+    a_piece(me, X).start()
+    up, down = d < nd - 1, d > 0
+
+    @pl.when(up)
+    def _():
+        a_piece(me, UP).start()
+
+    @pl.when(down)
+    def _():
+        a_piece(me, DOWN).start()
+
+    loads[3].wait()
+    h_across.start()
+    h_sib.start()
+    loads[4].wait()
+    loads[5].wait()
+
+    def positions_of(shard, index):
+        low = order[2 * shard] * half
+        high = order[2 * shard + 1] * half
+        return jnp.where(index < half, low + index, high + index - half)
+
+    place = positions_of(c, lax.broadcasted_iota(jnp.int32, (rows, HEAD_SIZE), 0)).astype(F32)
+    angle = place * freqs[...]
+    lane = lax.broadcasted_iota(jnp.int32, (rows, HEAD_SIZE), 1)
+    trig[0] = jnp.cos(angle)
+    sine = jnp.sin(angle)
+    trig[1] = jnp.where(lane < HEAD_SIZE // 2, -sine, sine)
+
+    def relay_a(s):
+        @pl.when(d >= s)
+        def _():
+            b = me - s
+            a_piece(b, DOWN).wait_recv()
+            a_piece(b, X).start()
+
+            @pl.when(up)
+            def _():
+                a_piece(b, UP).start()
+
+        @pl.when(d + s < nd)
+        def _():
+            b = me + s
+            a_piece(b, UP).wait_recv()
+            a_piece(b, X).start()
+
+            @pl.when(down)
+            def _():
+                a_piece(b, DOWN).start()
+
+    relay_a(1)
+
+    h_copy(across, 1, across).wait_recv()
+    h_relay.start()
+    h_copy(sibling, 0, sibling).wait_recv()
+    h_copy(diagonal, 2, sibling).wait_recv()
+    tp = xs.shape[0]
+    chunk = 64
+    per = wide // deep
+
+    def norm_rows(i, carry):
+        r = pl.multiple_of(i * chunk, chunk)
+        total = jnp.zeros((chunk, 1), F32)
+        for j in range(tp):
+            v = xs[j, pl.ds(r, chunk), :].astype(F32)
+            total = total + jnp.sum(v * v, axis=1, keepdims=True)
+        scale = lax.rsqrt(total * (1.0 / (tp * wide)) + 1e-05)
+        for j in range(tp):
+            for m in range(per):
+                v = xs[j, pl.ds(r, chunk), m * deep : (m + 1) * deep].astype(F32)
+                g = gain[:, j * wide + m * deep : j * wide + (m + 1) * deep]
+                normed[j * per + m, pl.ds(r, chunk), :] = (v * scale * g).astype(BF16)
+        return carry
+
+    lax.fori_loop(0, rows // chunk, norm_rows, 0)
+
+    for s in range(2, nd):
+        relay_a(s)
+        if s == nd - 2:
+
+            @pl.when(up)
+            def _():
+                o_piece(me, UP).start()
+
+            @pl.when(down)
+            def _():
+                o_piece(me, DOWN).start()
+
+    o_piece(me, X).start()
+    acc[...] = jnp.zeros_like(acc)
+
+    def project(b):
+        acc[...] += jnp.dot(normed[b], ga[b], preferred_element_type=F32)
+
+    def own_line(i, carry):
+        project(c * nd + i)
+        return carry
+
+    lax.fori_loop(0, nd, own_line, 0)
+
+    def relay_o_line(s):
+        @pl.when(d >= s)
+        def _():
+            b = me - s
+            o_piece(b, DOWN).wait_recv()
+
+            @pl.when(up)
+            def _():
+                o_piece(b, UP).start()
+
+        @pl.when(d + s < nd)
+        def _():
+            b = me + s
+            o_piece(b, UP).wait_recv()
+
+            @pl.when(down)
+            def _():
+                o_piece(b, DOWN).start()
+
+    def relay_o_x(s):
+        @pl.when((d >= s) & (d - s != e))
+        def _():
+            o_piece(me - s, X).start()
+
+        @pl.when((d + s < nd) & (d + s != e))
+        def _():
+            o_piece(me + s, X).start()
+
+    relay_o_line(1)
+
+    def other_line(i, carry):
+        far = jnp.where(d < nd // 2, i, nd - 1 - i)
+        b = (1 - c) * nd + far
+        a_piece(b, X).wait_recv()
+        project(b)
+        return carry
+
+    lax.fori_loop(0, nd, other_line, 0)
+
+    def rotated(v):
+        return (v * trig[0] + pltpu.roll(v, HEAD_SIZE // 2, 1) * trig[1]).astype(BF16)
+
+    kv[c, :, 0:HEAD_SIZE] = rotated(acc[:, qcols : qcols + HEAD_SIZE])
+    kv[c, :, HEAD_SIZE:] = acc[:, qcols + HEAD_SIZE :].astype(BF16)
+    kv_copy = remote(kv.at[c], kv.at[c], kv_send.at[0], kv_recv.at[0], {"ctx": 1 - c})
+    kv_copy.start()
+    relay_o_x(1)
+    for h in range(n_heads):
+        part = slice(h * HEAD_SIZE, (h + 1) * HEAD_SIZE)
+        query[h] = rotated(acc[:, part])
+    for s in range(2, nd):
+        relay_o_line(s)
+        relay_o_x(s)
+
+    mirror = (1 - c) * nd + d
+    o_piece(mirror, X).wait_recv()
+
+    @pl.when(d % 2 == 0)
+    def _():
+        o_piece(mirror, UP).start()
+
+    @pl.when(d % 2 == 1)
+    def _():
+        o_piece(mirror, DOWN).start()
+
+    remote(kv.at[1 - c], kv.at[1 - c], kv_send.at[0], kv_recv.at[0], {"ctx": 1 - c}).wait_recv()
+    qrows = 256
+    dims = (((1,), (1,)), ((), ()))
+
+    def attend_block(i, carry):
+        h = i // (rows // qrows)
+        r = pl.multiple_of((i % (rows // qrows)) * qrows, qrows)
+        q = query[h, pl.ds(r, qrows), :]
+        qpos = positions_of(c, r + lax.broadcasted_iota(jnp.int32, (qrows, rows), 0))
+        scores = []
+        for n in range(2):
+            kpos = positions_of(n, lax.broadcasted_iota(jnp.int32, (qrows, rows), 1))
+            sc = lax.dot_general(
+                q, kv[n, :, 0:HEAD_SIZE], dims, preferred_element_type=F32
+            ) * (1.0 / HEAD_SIZE**0.5)
+            scores.append(jnp.where(qpos >= kpos, sc, -1e30))
+        peak = jnp.maximum(
+            jnp.max(scores[0], axis=1, keepdims=True), jnp.max(scores[1], axis=1, keepdims=True)
+        )
+        total = jnp.zeros((qrows, 1), F32)
+        value = jnp.zeros((qrows, HEAD_SIZE), F32)
+        for n in range(2):
+            p = jnp.exp(scores[n] - peak)
+            total = total + jnp.sum(p, axis=1, keepdims=True)
+            value = value + jnp.dot(
+                p.astype(BF16), kv[n, :, HEAD_SIZE:], preferred_element_type=F32
+            )
+        attn[h, pl.ds(r, qrows), :] = (value / total).astype(BF16)
+        return carry
+
+    lax.fori_loop(0, n_heads * (rows // qrows), attend_block, 0)
+
+    js = nd // 2
+
+    def out_block(b):
+        full = jnp.concatenate([attn[h] for h in range(n_heads)], axis=1)
+        return jnp.dot(full, go[b], preferred_element_type=F32).astype(BF16)
+
+    def s_copy(side, j):
+        i = side * js + j
+        return block(sent, i, sib, i, s_send.at[i], s_recv.at[i], sibling)
+
+    def y_copy(j):
+        return block(ysend, j, yrecv, j, y_send.at[j], y_recv.at[j], across)
+
+    for phase in range(2):
+        side = c if phase == 0 else 1 - c
+
+        def ready(within):
+            if phase == 0:
+                return
+
+            @pl.when(within != d)
+            def _():
+                o_piece(side * nd + within, X).wait_recv()
+
+        def give(j, carry):
+            within = (1 - k) * js + j
+            ready(within)
+            sent[side * js + j] = out_block(side * nd + within)
+            s_copy(side, j).start()
+            return carry
+
+        def keep(j, carry):
+            within = k * js + j
+            ready(within)
+            kept[side * js + j] = out_block(side * nd + within)
+            s_copy(side, j).wait_recv()
+
+            @pl.when(side != y)
+            def _():
+                i = side * js + j
+                ysend[j] = (kept[i].astype(F32) + sib[i].astype(F32)).astype(BF16)
+                y_copy(j).start()
+
+            return carry
+
+        lax.fori_loop(0, js, give, 0)
+        lax.fori_loop(0, js, keep, 0)
+
+    cols = w_out.shape[1]
+    tile[...] = jnp.zeros_like(tile)
+    for j in range(js):
+        y_copy(j).wait_recv()
+
+        def finish(i, carry):
+            r = pl.multiple_of(i * chunk, chunk)
+            here = (pl.ds(r, chunk), slice(j * cols, (j + 1) * cols))
+            mine = y * js + j
+            rr = pl.ds(r, chunk)
+            total = (
+                kept[mine, rr, :].astype(F32) + sib[mine, rr, :].astype(F32)
+            ) + yrecv[j, rr, :].astype(F32)
+            result = total.astype(BF16)
+            out[here] = result
+            resid = xs[t, rr, j * cols : (j + 1) * cols].astype(F32) + result.astype(F32)
+            resid = resid - goal[rr, j * cols : (j + 1) * cols].astype(F32)
+            sq = jnp.sum((resid * resid).reshape(chunk // 8, 8, cols), axis=0)
+            part = sq[:, 0:128]
+            for m in range(1, cols // 128):
+                part = part + sq[:, m * 128 : (m + 1) * 128]
+            tile[...] += part
+            return carry
+
+        lax.fori_loop(0, rows // chunk, finish, 0)
+
+    sums_tp[0] = tile[...]
+    tp_copies = [
+        block(sums_tp, 0, sums_tp, 1 + i, t_send.at[i], t_recv.at[i], where)
+        for i, where in enumerate((sibling, across, diagonal))
+    ]
+    for copy in tp_copies:
+        copy.start()
+    for copy in tp_copies:
+        copy.wait_recv()
+    sums_all[me] = (sums_tp[0] + sums_tp[1]) + (sums_tp[2] + sums_tp[3])
+
+    def l_copy(s, slot):
+        p = (me + s) % nb
+        return remote(
+            sums_all.at[slot], sums_all.at[slot], l_send.at[s], l_recv.at[slot],
+            {"ctx": p // nd, "dp": p % nd},
+        )
+
+    for s in range(1, nb):
+        l_copy(s, me).start()
+    for s in range(1, nb):
+        l_copy(s, (me + s) % nb).wait_recv()
+    whole = sums_all[0]
+    for b in range(1, nb):
+        whole = whole + sums_all[b]
+    count = tp * wide * rows * nb
+    loss[...] = jnp.full(loss.shape, jnp.sum(whole) / count, F32)
+
+    h_across.wait_send()
+    h_sib.wait_send()
+    h_relay.wait_send()
+    kv_copy.wait_send()
+    for copy in tp_copies:
+        copy.wait_send()
+    for s in range(1, nb):
+        l_copy(s, me).wait_send()
+    for side in range(2):
+        for j in range(js):
+            s_copy(side, j).wait_send()
+    for j in range(js):
+        y_copy(j).wait_send()
+    a_piece(me, X).wait_send()
+    o_piece(me, X).wait_send()
+    for s in range(0, nd):
+        for sign in (-1, 1) if s else (1,):
+            b = me + sign * s
+            there = (d + sign * s >= 0) & (d + sign * s < nd)
+            if s:
+
+                @pl.when(there)
+                def _():
+                    a_piece(b, X).wait_send()
+
+                @pl.when(there & (d + sign * s != e))
+                def _():
+                    o_piece(b, X).wait_send()
+
+            if s == 0 or sign < 0:
+
+                @pl.when(there & up)
+                def _():
+                    a_piece(b, UP).wait_send()
+                    o_piece(b, UP).wait_send()
+
+            if s == 0 or sign > 0:
+
+                @pl.when(there & down)
+                def _():
+                    a_piece(b, DOWN).wait_send()
+                    o_piece(b, DOWN).wait_send()
+
+    @pl.when(d % 2 == 0)
+    def _():
+        o_piece(mirror, UP).wait_send()
+
+    @pl.when(d % 2 == 1)
+    def _():
+        o_piece(mirror, DOWN).wait_send()
+
+
+def fused(nd, hidden, target, gain, w_query, w_key, value_matrix, w_out, block_order):
+    rows, wide = hidden.shape[1:]
+    nb = 2 * nd
+    tp = lax.axis_size("tp")
+    deep, qcols = w_query.shape
+    all_cols = qcols + w_key.shape[1] + value_matrix.shape[1]
+    orows, ocols = w_out.shape
+    half = HEAD_SIZE // 2
+    freqs = rope_base ** (-(jnp.arange(half, dtype=F32) * 2.0) / HEAD_SIZE)
+    freqs = jnp.concatenate([freqs, freqs])[None, :]
+    heads = qcols // HEAD_SIZE
+    js = nd // 2
+    vmem = pl.BlockSpec(memory_space=pltpu.VMEM)
+    anyspace = pl.BlockSpec(memory_space=pl.ANY)
+    dma = pltpu.SemaphoreType.DMA
+    branch, loss = pl.pallas_call(
+        functools.partial(layer, nd),
+        out_shape=(
+            jax.ShapeDtypeStruct((rows, wide), BF16),
+            jax.ShapeDtypeStruct((8, 128), F32),
+        ),
+        in_specs=[
+            pl.BlockSpec(memory_space=pltpu.SMEM),
+            anyspace,
+            anyspace,
+            vmem,
+            vmem,
+            anyspace,
+            anyspace,
+            anyspace,
+            anyspace,
+        ],
+        out_specs=(vmem, vmem),
+        scratch_shapes=[
+            pltpu.VMEM((nb, deep, all_cols), BF16),
+            pltpu.VMEM((nb, orows, ocols), BF16),
+            pltpu.VMEM((tp, rows, wide), BF16),
+            pltpu.VMEM((rows, wide), BF16),
+            pltpu.VMEM((nb, rows, deep), BF16),
+            pltpu.VMEM((rows, all_cols), F32),
+            pltpu.VMEM((2, rows, HEAD_SIZE), F32),
+            pltpu.VMEM((heads, rows, HEAD_SIZE), BF16),
+            pltpu.VMEM((2, rows, 2 * HEAD_SIZE), BF16),
+            pltpu.VMEM((heads, rows, HEAD_SIZE), BF16),
+            pltpu.VMEM((2 * js, rows, ocols), BF16),
+            pltpu.VMEM((2 * js, rows, ocols), BF16),
+            pltpu.VMEM((2 * js, rows, ocols), BF16),
+            pltpu.VMEM((js, rows, ocols), BF16),
+            pltpu.VMEM((js, rows, ocols), BF16),
+            pltpu.VMEM((8, 128), F32),
+            pltpu.VMEM((tp, 8, 128), F32),
+            pltpu.VMEM((nb, 8, 128), F32),
+            dma((6,)),
+            dma((3, nb)),
+            dma((nb,)),
+            dma((3, nb)),
+            dma((nb,)),
+            dma((3,)),
+            dma((3,)),
+            dma((1,)),
+            dma((1,)),
+            dma((2 * js,)),
+            dma((2 * js,)),
+            dma((js,)),
+            dma((js,)),
+            dma((3,)),
+            dma((3,)),
+            dma((nb,)),
+            dma((nb,)),
+        ],
+        compiler_params=pltpu.CompilerParams(
+            collective_id=1, has_side_effects=True, vmem_limit_bytes=60 * 1024 * 1024
+        ),
+    )(
+        block_order,
+        hidden[0],
+        target[0],
+        gain[None, :],
+        freqs,
+        w_query,
+        w_key,
+        value_matrix,
+        w_out,
+    )
+    return (branch[None], loss[0, 0])
+
+
 def solution(mesh):
     in_specs = (
         P("dp", "ctx", "tp"),
@@ -141,6 +707,9 @@
         P(),
     )
     out_specs = (P("dp", "ctx", "tp"), P())
+    sizes = mesh.shape
+    fits = sizes["ctx"] == 2 and sizes["tp"] == 4 and sizes["dp"] % 2 == 0
+    body = functools.partial(fused, sizes["dp"]) if fits else on_device
     return jax.shard_map(
-        on_device, mesh=mesh, in_specs=in_specs, out_specs=out_specs, check_vma=False
-    )
+        body, mesh=mesh, in_specs=in_specs, out_specs=out_specs, check_vma=False
+    )

time: 379 us -> 153 us (0.40)
  waiting for transfers between devices: 281 us -> 0 us
  Pallas kernels: 0 us -> 148 us
  blocking collectives: 39.5 us -> 0 us
  matrix products: 27.6 us -> 0 us
  between operations: 16.1 us -> 0.64 us
  other arithmetic: 13.3 us -> 0.6 us
    all_gather x5 -> x0, waiting for transfers between devices: 235 us -> none  [the longest x1 68.1 us: on_device(): lax.all_gather(w_query, ('ctx', 'dp'), axis=0, tiled=True)]
    pallas_call x0 -> x1, Pallas kernels: none -> 148 us  [fused(): pl.pallas_call(functools.partial(layer, nd), out_shape=(jax.ShapeDtypeStr...]
    reduce_scatter x1 -> x0, waiting for transfers between devices: 42.7 us -> none  [on_device(): lax.psum_scatter(terms.astype(jnp.bfloat16), 'tp', scatter_dimension=1, t...]
    psum x1 -> x0, blocking collectives: 39.5 us -> none  [on_device(): squares = lax.psum(jnp.sum(resid * resid), ('ctx', 'tp', 'dp'))]
    dot_general x8 -> x0, matrix products: 27.6 us -> none  [the longest x3 14.1 us: on_device(): jnp.dot(normed, piece, preferred_element_type=jnp.float32)]
    reduce_sum x5 -> x0, other arithmetic: 8.47 us -> none  [the longest x1 3.08 us: on_device(): jnp.mean(wide * wide, axis=1, keepdims=True) + 1e-05]
  transfers between devices with their start and end apart: 7 -> 0, of which waited for: 6 -> 0; matrix products, arithmetic and copies ran while one was open for 9% -> 0% of each run, Pallas kernels for 0% -> 0%
where the time goes in v1:
time: 153 us; the launch traced here: 152 us
  Pallas kernels  148 us (97%)
  local copies, waits for them, and re-layouts  3.45 us (2%)
    pallas_call x1, Pallas kernels, fused(): pl.pallas_call(functools.partial(layer, nd), out_shape=(jax.ShapeDtypeStr...  148 us

profile of v1, /device:TPU:0, one launch (start us, length us, event | category | flops | bytes accessed | tf_op | source)
XLA Modules:
  0.0 152.4 jit_solution(2995950784810181786)
XLA Ops:
  0.6 0.6 maximum_bitcast_fusion.freqs
  1.2 147.7 %shard_map.95 = (bf16[512,1024]{1,0:T(8,128)(2,1)}, f32[8,128]{1,0:T(8,128)}) custom-call(s32[4]{0:T(128)} %order.1, bf16[512,1024]{1,0:T(8,128)(2,1)} %bitcast.7, bf16[512,1024]{1,0:T(8,128)(2,1)} %bitcast.8, f32[1,4096]{1,0:T(1,128)} %bitcast.10, f32[1,128]{1,0:T(1,128)} %maximum_bitcast_fusion.freqs, bf16[512,512]{1,0:T(8,128)(2,1)} %w_query.1, ...), custom_call_target="tpu_custom_call" | custom-call | tf_op jit(solution)/shard_map/pallas_call | solution.py:626
  148.9 1.2 slice.3
  150.1 2.3 %copy.11 = bf16[1,512,1024]{2,1,0:T(8,128)(2,1)} copy(bf16[1,512,1024]{2,1,0:T(8,128)(2,1)} %bitcast.9) | data formatting | bytes 2097152
  (1 shorter events, 0.0 us)

commit v2 on v1

--- a/solution.py
+++ b/solution.py
@@ -467,66 +467,77 @@
     def y_copy(j):
         return block(ysend, j, yrecv, j, y_send.at[j], y_recv.at[j], across)
 
+    near = d < js
+
+    def arrival(i):
+        pair, r = i // 2, i % 2
+        group = (d // 2 + pair) % js
+        mine = jnp.where(r == 0, d, e)
+        return jnp.where(pair == 0, mine, group * 2 + jnp.where(near, r, 1 - r))
+
     for phase in range(2):
         side = c if phase == 0 else 1 - c
 
-        def ready(within):
-            if phase == 0:
-                return
-
-            @pl.when(within != d)
+        def columns(i, carry):
+            within = arrival(i)
+            if phase == 1:
+
+                @pl.when(within != d)
+                def _():
+                    o_piece(side * nd + within, X).wait_recv()
+
+            j = within % js
+            slot = side * js + j
+            value = out_block(side * nd + within)
+            own = within // js == k
+
+            @pl.when(jnp.logical_not(own))
             def _():
-                o_piece(side * nd + within, X).wait_recv()
-
-        def give(j, carry):
-            within = (1 - k) * js + j
-            ready(within)
-            sent[side * js + j] = out_block(side * nd + within)
-            s_copy(side, j).start()
+                sent[slot] = value
+                s_copy(side, j).start()
+
+            @pl.when(own)
+            def _():
+                kept[slot] = value
+                s_copy(side, j).wait_recv()
+
+                @pl.when(side != y)
+                def _():
+                    ysend[j] = (kept[slot].astype(F32) + sib[slot].astype(F32)).astype(BF16)
+                    y_copy(j).start()
+
             return carry
 
-        def keep(j, carry):
-            within = k * js + j
-            ready(within)
-            kept[side * js + j] = out_block(side * nd + within)
-            s_copy(side, j).wait_recv()
-
-            @pl.when(side != y)
-            def _():
-                i = side * js + j
-                ysend[j] = (kept[i].astype(F32) + sib[i].astype(F32)).astype(BF16)
-                y_copy(j).start()
-
-            return carry
-
-        lax.fori_loop(0, js, give, 0)
-        lax.fori_loop(0, js, keep, 0)
+        lax.fori_loop(0, nd, columns, 0)
 
     cols = w_out.shape[1]
     tile[...] = jnp.zeros_like(tile)
-    for j in range(js):
+    def finish_block(n, carry):
+        j = jnp.where(near, n, js - 1 - n)
         y_copy(j).wait_recv()
-
-        def finish(i, carry):
-            r = pl.multiple_of(i * chunk, chunk)
-            here = (pl.ds(r, chunk), slice(j * cols, (j + 1) * cols))
-            mine = y * js + j
-            rr = pl.ds(r, chunk)
+        place = pl.ds(pl.multiple_of(j * cols, cols), cols)
+        mine = y * js + j
+
+        def finish(i, inner):
+            rr = pl.ds(pl.multiple_of(i * chunk, chunk), chunk)
             total = (
                 kept[mine, rr, :].astype(F32) + sib[mine, rr, :].astype(F32)
             ) + yrecv[j, rr, :].astype(F32)
             result = total.astype(BF16)
-            out[here] = result
-            resid = xs[t, rr, j * cols : (j + 1) * cols].astype(F32) + result.astype(F32)
-            resid = resid - goal[rr, j * cols : (j + 1) * cols].astype(F32)
+            out[rr, place] = result
+            resid = xs[t, rr, place].astype(F32) + result.astype(F32)
+            resid = resid - goal[rr, place].astype(F32)
             sq = jnp.sum((resid * resid).reshape(chunk // 8, 8, cols), axis=0)
             part = sq[:, 0:128]
             for m in range(1, cols // 128):
                 part = part + sq[:, m * 128 : (m + 1) * 128]
             tile[...] += part
-            return carry
+            return inner
 
         lax.fori_loop(0, rows // chunk, finish, 0)
+        return carry
+
+    lax.fori_loop(0, js, finish_block, 0)
 
     sums_tp[0] = tile[...]
     tp_copies = [
@@ -554,7 +565,7 @@
     for b in range(1, nb):
         whole = whole + sums_all[b]
     count = tp * wide * rows * nb
-    loss[...] = jnp.full(loss.shape, jnp.sum(whole) / count, F32)
+    loss[0, 0] = jnp.sum(whole) / count
 
     h_across.wait_send()
     h_sib.wait_send()
@@ -627,7 +638,7 @@
         functools.partial(layer, nd),
         out_shape=(
             jax.ShapeDtypeStruct((rows, wide), BF16),
-            jax.ShapeDtypeStruct((8, 128), F32),
+            jax.ShapeDtypeStruct((1, 1), F32),
         ),
         in_specs=[
             pl.BlockSpec(memory_space=pltpu.SMEM),
@@ -640,7 +651,7 @@
             anyspace,
             anyspace,
         ],
-        out_specs=(vmem, vmem),
+        out_specs=(vmem, pl.BlockSpec(memory_space=pltpu.SMEM)),
         scratch_shapes=[
             pltpu.VMEM((nb, deep, all_cols), BF16),
             pltpu.VMEM((nb, orows, ocols), BF16),
@@ -692,7 +703,7 @@
         value_matrix,
         w_out,
     )
-    return (branch[None], loss[0, 0])
+    return (branch[None], loss.reshape(()))
 
 
 def solution(mesh):

time: 153 us -> 151 us (0.987)
  Pallas kernels: 148 us -> 145 us
  between operations: 0.64 us -> 2.33 us
    pallas_call x1, Pallas kernels: 148 us -> 145 us  [fused(): pl.pallas_call(functools.partial(layer, nd), out_shape=(jax.ShapeDtypeStr...]
where the time goes in v2:
time: 151 us; the launch traced here: 150 us
  Pallas kernels  145 us (96%)
  between operations  2.33 us (2%)
  local copies, waits for them, and re-layouts  2.26 us (1%)
    pallas_call x1, Pallas kernels, fused(): pl.pallas_call(functools.partial(layer, nd), out_shape=(jax.ShapeDtypeStr...  145 us

profile of v2, /device:TPU:0, one launch (start us, length us, event | category | flops | bytes accessed | tf_op | source)
XLA Modules:
  0.0 150.3 jit_solution(14331552166951309923)
XLA Ops:
  0.6 0.6 maximum_bitcast_fusion.freqs
  1.2 145.1 %shard_map.95 = (bf16[512,1024]{1,0:T(8,128)(2,1)}, f32[1,1]{1,0:T(1,128)}) custom-call(s32[4]{0:T(128)} %order.1, bf16[512,1024]{1,0:T(8,128)(2,1)} %bitcast.7, bf16[512,1024]{1,0:T(8,128)(2,1)} %bitcast.8, f32[1,4096]{1,0:T(1,128)} %bitcast.10, f32[1,128]{1,0:T(1,128)} %maximum_bitcast_fusion.freqs, bf16[512,512]{1,0:T(8,128)(2,1)} %w_query.1, ...), custom_call_target="tpu_custom_call" | custom-call | tf_op jit(solution)/shard_map/pallas_call | solution.py:637
  146.4 2.3 %copy.12 = bf16[1,512,1024]{2,1,0:T(8,128)(2,1)} copy(bf16[1,512,1024]{2,1,0:T(8,128)(2,1)} %bitcast.9) | data formatting | bytes 2097152
  (1 shorter events, 0.0 us)

commit v3 on v2

--- a/solution.py
+++ b/solution.py
@@ -345,7 +345,6 @@
             def _():
                 o_piece(me, DOWN).start()
 
-    o_piece(me, X).start()
     acc[...] = jnp.zeros_like(acc)
 
     def project(b):
@@ -403,24 +402,14 @@
     kv[c, :, HEAD_SIZE:] = acc[:, qcols + HEAD_SIZE :].astype(BF16)
     kv_copy = remote(kv.at[c], kv.at[c], kv_send.at[0], kv_recv.at[0], {"ctx": 1 - c})
     kv_copy.start()
+    o_piece(me, X).start()
     relay_o_x(1)
     for h in range(n_heads):
         part = slice(h * HEAD_SIZE, (h + 1) * HEAD_SIZE)
         query[h] = rotated(acc[:, part])
-    for s in range(2, nd):
+    for s in range(2, nd - 1):
         relay_o_line(s)
         relay_o_x(s)
-
-    mirror = (1 - c) * nd + d
-    o_piece(mirror, X).wait_recv()
-
-    @pl.when(d % 2 == 0)
-    def _():
-        o_piece(mirror, UP).start()
-
-    @pl.when(d % 2 == 1)
-    def _():
-        o_piece(mirror, DOWN).start()
 
     remote(kv.at[1 - c], kv.at[1 - c], kv_send.at[0], kv_recv.at[0], {"ctx": 1 - c}).wait_recv()
     qrows = 256
@@ -453,6 +442,21 @@
         return carry
 
     lax.fori_loop(0, n_heads * (rows // qrows), attend_block, 0)
+
+    for s in range(max(2, nd - 1), nd):
+        relay_o_line(s)
+        relay_o_x(s)
+
+    mirror = (1 - c) * nd + d
+    o_piece(mirror, X).wait_recv()
+
+    @pl.when(d % 2 == 0)
+    def _():
+        o_piece(mirror, UP).start()
+
+    @pl.when(d % 2 == 1)
+    def _():
+        o_piece(mirror, DOWN).start()
 
     js = nd // 2
 

time: 151 us -> 146 us (0.967)
  Pallas kernels: 145 us -> 141 us
    pallas_call x1, Pallas kernels: 145 us -> 141 us  [fused(): pl.pallas_call(functools.partial(layer, nd), out_shape=(jax.ShapeDtypeStr...]
where the time goes in v3:
time: 146 us
  Pallas kernels  141 us (97%)
  between operations  2.33 us (2%)
  local copies, waits for them, and re-layouts  2.26 us (2%)
    pallas_call x1, Pallas kernels, fused(): pl.pallas_call(functools.partial(layer, nd), out_shape=(jax.ShapeDtypeStr...  141 us

profile of v3, /device:TPU:0, one launch (start us, length us, event | category | flops | bytes accessed | tf_op | source)
XLA Modules:
  0.0 145.7 jit_solution(16058681304099059124)
XLA Ops:
  0.6 0.6 maximum_bitcast_fusion.freqs
  1.2 140.5 %shard_map.95 = (bf16[512,1024]{1,0:T(8,128)(2,1)}, f32[1,1]{1,0:T(1,128)}) custom-call(s32[4]{0:T(128)} %order.1, bf16[512,1024]{1,0:T(8,128)(2,1)} %bitcast.7, bf16[512,1024]{1,0:T(8,128)(2,1)} %bitcast.8, f32[1,4096]{1,0:T(1,128)} %bitcast.10, f32[1,128]{1,0:T(1,128)} %maximum_bitcast_fusion.freqs, bf16[512,512]{1,0:T(8,128)(2,1)} %w_query.1, ...), custom_call_target="tpu_custom_call" | custom-call | tf_op jit(solution)/shard_map/pallas_call | solution.py:641
  141.8 2.3 %copy.12 = bf16[1,512,1024]{2,1,0:T(8,128)(2,1)} copy(bf16[1,512,1024]{2,1,0:T(8,128)(2,1)} %bitcast.9) | data formatting | bytes 2097152
  (1 shorter events, 0.0 us)
